TPU v7x, 32 devices: a whole 2x2x4 slice. The times are simulated.
32 devices in a mesh: row: 8 (over z, core), col: 4 (over y, x).
Axes of the slice: x: 2, y: 2, z: 4, core: 2. Of those that a mesh axis runs over, the one named last changes fastest.
Arguments:
- x_fwd: bfloat16 [512, 6144], P('row', 'col'), may hold values from -6 to 6
- x_bwd: bfloat16 [512, 6144], P('row', 'col'), may hold values from -6 to 6
- grad_out: bfloat16 [512, 6144], P('row', 'col'), may hold values from -1.5 to 1.5
- gain: float32 [6144], P('col'), may hold values from 0.1 to 1.9
- w_up: bfloat16 [6144, 12288], P('col', 'row'), may hold values from -0.078125 to 0.078125
- w_down: bfloat16 [12288, 6144], P('row', 'col'), may hold values from -0.0546875 to 0.0546875
Outputs:
- y_fwd: bfloat16 [512, 6144], P('row', 'col')
- dx_bwd: bfloat16 [512, 6144], P('row', 'col')
- step_up: float32 [6144, 12288], P('col', 'row')
- step_down: float32 [12288, 6144], P('row', 'col')
- step_gain: float32 [6144], P('col')
- grad_rms: float32 [], replicated
All inputs are finite; a program needn't handle non-finite values.
Results may differ from a plain program's by a relative error of at most 0.0017.
The roundings to bfloat16 on the way count: a program that leaves them out, or rounds other values in their place, can miss the bound.
Values may be sent and summed in bfloat16 or wider, within the bound.
A program may use at most 128 MiB of HBM per device.

v0:
```python
import math
import jax
import jax.numpy as jnp
from jax import lax
from jax.sharding import PartitionSpec as P

D = 6144
FF = 12288
eps = 1e-06
clip_share = 0.25


def erf_gelu(value):
    return 0.5 * value * (1.0 + lax.erf(value * 0.7071067811865476))


def gelu_slope(value):
    return (
        0.5 * (1.0 + lax.erf(value * 0.7071067811865476))
        + value * jnp.exp(-0.5 * value * value) * 0.3989422804014327
    )


def contract(left, right, left_dim, right_dim):
    return lax.dot_general(
        left, right, (((left_dim,), (right_dim,)), ((), ())), preferred_element_type=jnp.float32
    )


def row_sums(tokens):
    values = tokens.astype(jnp.float32)
    return (jnp.sum(values, -1), jnp.sum(values * values, -1))


def normalize(tokens, first, second):
    values = tokens.astype(jnp.float32)
    centre = first / D
    spread = second / D - centre * centre
    inv_scale = lax.rsqrt(spread + eps)
    return ((values - centre[:, None]) * inv_scale[:, None], inv_scale)


def up_both(normed_a, normed_b, w_up):
    full_a, full_b = (
        lax.all_gather(normed_a, "row", axis=0, tiled=True),
        lax.all_gather(normed_b, "row", axis=0, tiled=True),
    )
    width = w_up.shape[1]
    summed = lax.psum_scatter(
        jnp.concatenate(
            [
                jnp.dot(full_a, w_up, preferred_element_type=jnp.float32),
                jnp.dot(full_b, w_up, preferred_element_type=jnp.float32),
            ],
            1,
        ),
        "col",
        scatter_dimension=0,
        tiled=True,
    )
    return (summed[:, :width], summed[:, width:], full_b)


def on_device(x_fwd, x_bwd, grad_out, gain, w_up, w_down):
    first_a, second_a = row_sums(x_fwd)
    first_b, second_b = row_sums(x_bwd)
    first_a, second_a, first_b, second_b = lax.psum((first_a, second_a, first_b, second_b), "col")
    centred_a, _ = normalize(x_fwd, first_a, second_a)
    centred_b, inv_scale = normalize(x_bwd, first_b, second_b)
    normed_a = (centred_a * gain).astype(jnp.bfloat16)
    normed_b = (centred_b * gain).astype(jnp.bfloat16)
    pre_a, pre_b, normed_full = up_both(normed_a, normed_b, w_up)
    hidden_a = erf_gelu(pre_a).astype(jnp.bfloat16)
    output_part = jnp.dot(
        lax.all_gather(hidden_a, "col", axis=0, tiled=True),
        w_down,
        preferred_element_type=jnp.float32,
    )
    output_sum = lax.psum_scatter(output_part, "row", scatter_dimension=0, tiled=True)
    y_fwd = (x_fwd.astype(jnp.float32) + output_sum).astype(jnp.bfloat16)
    hidden_b = erf_gelu(pre_b).astype(jnp.bfloat16)
    grad_full = lax.all_gather(grad_out, "row", axis=0, tiled=True)
    grad_hidden = lax.psum_scatter(
        contract(grad_full, w_down, 1, 1), "col", scatter_dimension=0, tiled=True
    )
    grad_pre = (grad_hidden * gelu_slope(pre_b)).astype(jnp.bfloat16)
    hidden_piece = lax.all_gather(hidden_b, "col", axis=0, tiled=True)
    pre_piece = lax.all_gather(grad_pre, "col", axis=0, tiled=True)
    down_total = contract(hidden_piece, grad_full, 0, 0)
    up_total = contract(normed_full, pre_piece, 0, 0)
    input_total = contract(pre_piece, w_up, 1, 1)
    grad_normed = lax.psum_scatter(input_total, "row", scatter_dimension=0, tiled=True)
    scaled = grad_normed * gain
    first_back = jnp.sum(scaled, -1)
    second_back = jnp.sum(scaled * centred_b, -1)
    first_back, second_back = lax.psum((first_back, second_back), "col")
    dx_bwd = (
        grad_out.astype(jnp.float32)
        + inv_scale[:, None]
        * (scaled - first_back[:, None] / D - centred_b * (second_back[:, None] / D))
    ).astype(jnp.bfloat16)
    gain_part = jnp.sum(grad_normed * centred_b, 0)
    weight_squares = jnp.sum(up_total * up_total) + jnp.sum(down_total * down_total)
    g_gain = lax.psum(gain_part, "row")
    first_row = (lax.axis_index("row") == 0).astype(jnp.float32)
    total = lax.psum(weight_squares + first_row * jnp.sum(g_gain * g_gain), ("row", "col"))
    param_count = 2 * D * FF + D
    norm_value = jnp.sqrt(total)
    grad_rms = norm_value / math.sqrt(param_count)
    factor = jnp.minimum(1.0, clip_share * math.sqrt(param_count) / norm_value)
    return (y_fwd, dx_bwd, up_total * factor, down_total * factor, g_gain * factor, grad_rms)


def solution(mesh):
    placed = (
        P("row", "col"),
        P("row", "col"),
        P("row", "col"),
        P("col"),
        P("col", "row"),
        P("row", "col"),
    )
    return jax.shard_map(
        on_device,
        mesh=mesh,
        in_specs=placed,
        out_specs=(
            P("row", "col"),
            P("row", "col"),
            P("col", "row"),
            P("row", "col"),
            P("col"),
            P(),
        ),
        check_vma=False,
    )
```

profile of v0, /device:TPU:0, one launch (start us, length us, event | category | flops | bytes accessed | tf_op | source)
XLA Modules:
  0.0 446.6 jit_solution(12459251885347289089)
XLA Ops:
  7.2 0.0 all-gather.13.cloned.1.call-start
  7.2 0.7 all-gather.13.cloned.1.call-update
  7.9 0.0 all-gather.7.cloned.1.call-start
  7.9 1.1 convert_reduce_fusion
  9.0 1.1 convert_reduce_fusion.1
  10.1 11.4 %all-reduce.1 = (f32[64]{0:T(128)S(1)}, f32[64]{0:T(128)S(1)}, f32[64]{0:T(128)S(1)}, f32[64]{0:T(128)S(1)}) all-reduce(f32[64]{0:T(128)S(1)} %get-tuple-element.12, f32[64]{0:T(128)S(1)} %get-tuple-element.11, f32[64]{0:T(128)S(1)} %get-tuple-element.10, f32[64]{0:T(128)S(1)} %get-tuple-element.9), channel_id=1, replica_groups=mesh['row'=8,'col'=4] {'col'}, use_global_device_ids=true, to_apply=%region_7.0 | all-reduce | flops 256 | bytes 2048 | tf_op jit(solution)/shard_map/psum | solution.py:67
  21.5 2.0 fusion.21
  23.6 0.0 all-gather.7.cloned.1.call-update
  23.6 0.0 all-gather.9.cloned.1.call-start
  23.6 0.7 all-gather.9.cloned.1.call-update
  24.3 0.0 reduce-scatter.9.cloned.1.call-start
  24.4 13.3 %all-gather.13.cloned.1.call-done = bf16[512,1536]{1,0:T(8,128)(2,1)} async-done(((bf16[64,1536]{1,0:T(8,128)(2,1)}), bf16[512,1536]{1,0:T(8,128)(2,1)}) %all-gather.13.cloned.1.call-update) | async-done | bytes 1572880 | tf_op jit(solution)/shard_map/all_gather | solution.py:82
  37.6 7.1 %fusion.27 = f32[512,1536]{1,0:T(8,128)} fusion(bf16[512,1536]{1,0:T(8,128)(2,1)} %all-gather.13.cloned.1.call-done, bf16[1536,1536]{1,0:T(8,128)(2,1)} %param.11), kind=kOutput, calls=%fused_computation.52 | convolution fusion | flops 2415919104 | bytes 9437184 | tf_op jit(solution)/shard_map/dot_general | solution.py:25
  44.8 0.0 reduce-scatter.9.cloned.1.call-update
  44.8 0.0 reduce-scatter.5.cloned.1.call-start
  44.8 19.4 %all-gather.7.cloned.1.call-done = bf16[512,1536]{1,0:T(8,128)(2,1)} async-done(((bf16[64,1536]{1,0:T(8,128)(2,1)}), bf16[512,1536]{1,0:T(8,128)(2,1)}) %all-gather.7.cloned.1.call-update) | async-done | bytes 1572880 | tf_op jit(solution)/shard_map/all_gather | solution.py:45
  64.3 4.9 %fusion.24 = f32[512,1536]{1,0:T(8,128)S(1)} fusion(bf16[512,1536]{1,0:T(8,128)(2,1)} %all-gather.7.cloned.1.call-done, bf16[1536,1536]{1,0:T(8,128)(2,1)} %param.10), kind=kOutput, calls=%fused_computation.49 | convolution fusion | flops 2415919104 | bytes 9437184 | tf_op jit(solution)/shard_map/dot_general | solution.py:52
  69.2 21.7 %all-gather.9.cloned.1.call-done = bf16[512,1536]{1,0:T(8,128)(2,1)} async-done(((bf16[64,1536]{1,0:T(8,128)(2,1)}), bf16[512,1536]{1,0:T(8,128)(2,1)}) %all-gather.9.cloned.1.call-update) | async-done | bytes 1572880 | tf_op jit(solution)/shard_map/all_gather | solution.py:46
  90.9 4.9 %fusion.25 = f32[512,1536]{1,0:T(8,128)S(1)} fusion(bf16[512,1536]{1,0:T(8,128)(2,1)} %all-gather.9.cloned.1.call-done, bf16[1536,1536]{1,0:T(8,128)(2,1)} %param.10), kind=kOutput, calls=%fused_computation.50 | convolution fusion | flops 2415919104 | bytes 9437184 | tf_op jit(solution)/shard_map/dot_general | solution.py:53
  95.9 3.3 pad_maximum_fusion
  99.1 0.0 reduce-scatter.5.cloned.1.call-update
  99.1 0.0 all-gather.15.cloned.1.call-start
  99.2 38.2 %reduce-scatter.9.cloned.1.call-done = f32[128,1536]{1,0:T(8,128)} async-done(((f32[512,1536]{1,0:T(8,128)}), f32[128,1536]{1,0:T(8,128)}) %reduce-scatter.9.cloned.1.call-update) | async-done | bytes 786448 | tf_op jit(solution)/shard_map/reduce_scatter | solution.py:83
  137.4 73.5 %reduce-scatter.5.cloned.1.call-done = f32[128,3072]{1,0:T(8,128)} async-done(((f32[512,3072]{1,0:T(8,128)}), f32[128,3072]{1,0:T(8,128)}) %reduce-scatter.5.cloned.1.call-update) | async-done | bytes 1572880 | tf_op jit(solution)/shard_map/reduce_scatter | solution.py:49
  210.9 3.0 multiply_convert_fusion
  213.9 0.0 all-gather.15.cloned.1.call-update
  213.9 0.0 all-gather.11.cloned.1.call-start
  214.0 0.7 all-gather.11.cloned.1.call-update
  214.7 0.0 all-gather.17.cloned.1.call-start
  214.7 0.7 all-gather.17.cloned.1.call-update
  215.4 0.0 reduce-scatter.11.cloned.1.call-start
  215.5 29.5 %all-gather.15.cloned.1.call-done = bf16[512,1536]{1,0:T(8,128)(2,1)} async-done(((bf16[128,1536]{1,0:T(8,128)(2,1)}), bf16[512,1536]{1,0:T(8,128)(2,1)}) %all-gather.15.cloned.1.call-update) | async-done | bytes 1572880 | tf_op jit(solution)/shard_map/all_gather | solution.py:88
  244.9 7.1 %fusion.28 = f32[512,1536]{1,0:T(8,128)} fusion(bf16[512,1536]{1,0:T(8,128)(2,1)} %all-gather.15.cloned.1.call-done, bf16[1536,1536]{1,0:T(8,128)(2,1)} %param.10), kind=kOutput, calls=%fused_computation.53 | convolution fusion | flops 2415919104 | bytes 9437184 | tf_op jit(solution)/shard_map/dot_general | solution.py:25
  252.0 0.0 reduce-scatter.11.cloned.1.call-update
  252.1 0.2 reduce-scatter.7.cloned.1.call-start
  252.3 25.3 %all-gather.11.cloned.1.call-done = bf16[512,1536]{1,0:T(8,128)(2,1)} async-done(((bf16[128,1536]{1,0:T(8,128)(2,1)}), bf16[512,1536]{1,0:T(8,128)(2,1)}) %all-gather.11.cloned.1.call-update) | async-done | bytes 1572880 | tf_op jit(solution)/shard_map/all_gather | solution.py:75
  277.6 7.1 %fusion.26 = f32[512,1536]{1,0:T(8,128)} fusion(bf16[512,1536]{1,0:T(8,128)(2,1)} %all-gather.11.cloned.1.call-done, bf16[1536,1536]{1,0:T(8,128)(2,1)} %param.11), kind=kOutput, calls=%fused_computation.51 | convolution fusion | flops 2415919104 | bytes 9437184 | tf_op jit(solution)/shard_map/dot_general | solution.py:74
  284.8 0.0 reduce-scatter.7.cloned.1.call-update
  284.8 1.4 copy-done.5
  286.2 0.5 copy-done.6
  286.7 6.0 %multiply_reduce_fusion.1 = (f32[]{:T(128)}, f32[1536,1536]{1,0:T(8,128)}) fusion(bf16[512,1536]{1,0:T(8,128)(2,1)S(1)} %copy-done.5, bf16[512,1536]{1,0:T(8,128)(2,1)S(1)} %copy-done.6), kind=kOutput, calls=%fused_computation.1 | convolution fusion | flops 2420637696 | bytes 12582916 | tf_op jit(solution)/shard_map/dot_general | solution.py:25
  292.7 18.2 %all-gather.17.cloned.1.call-done = bf16[512,1536]{1,0:T(8,128)(2,1)} async-done(((bf16[128,1536]{1,0:T(8,128)(2,1)}), bf16[512,1536]{1,0:T(8,128)(2,1)}) %all-gather.17.cloned.1.call-update) | async-done | bytes 1572880 | tf_op jit(solution)/shard_map/all_gather | solution.py:87
  310.9 8.9 %multiply_reduce_fusion = (f32[]{:T(128)}, f32[1536,1536]{1,0:T(8,128)}) fusion(bf16[512,1536]{1,0:T(8,128)(2,1)} %all-gather.17.cloned.1.call-done, bf16[512,1536]{1,0:T(8,128)(2,1)} %all-gather.13.cloned.1.call-done), kind=kOutput, calls=%fused_computation | convolution fusion | flops 2420637696 | bytes 12582916 | tf_op jit(solution)/shard_map/dot_general | solution.py:25
  321.1 32.5 %reduce-scatter.11.cloned.1.call-done = f32[64,1536]{1,0:T(8,128)} async-done(((f32[512,1536]{1,0:T(8,128)}), f32[64,1536]{1,0:T(8,128)}) %reduce-scatter.11.cloned.1.call-update) | async-done | bytes 393232 | tf_op jit(solution)/shard_map/reduce_scatter | solution.py:92
  353.6 0.0 copy-done
  353.6 0.0 copy-done.4
  353.6 1.4 fusion.17
  355.0 16.1 %psum.62 = f32[1536]{0:T(1024)S(1)} all-reduce(f32[1536]{0:T(1024)S(1)} %get-tuple-element.6), channel_id=1, replica_groups=mesh['row'=8,'col'=4] {'row'}, use_global_device_ids=true, to_apply=%region_19.0 | all-reduce | flops 1536 | bytes 12288 | tf_op jit(solution)/shard_map/psum | solution.py:104
  371.1 0.6 multiply_reduce_fusion.3
  372.3 38.8 %psum.63 = f32[]{:T(128)} all-reduce(f32[]{:T(128)S(6)} %add.60), channel_id=1, replica_groups=mesh['row'=8,'col'=4] {'row','col'}, use_global_device_ids=true, to_apply=%region_21.0 | all-reduce | flops 1 | bytes 8 | tf_op jit(solution)/shard_map/psum | solution.py:106
  411.9 9.9 %all-reduce = (f32[64]{0:T(128)S(1)}, f32[64]{0:T(128)S(1)}) all-reduce(f32[64]{0:T(128)S(1)} %get-tuple-element.7, f32[64]{0:T(128)S(1)} %get-tuple-element.8), channel_id=1, replica_groups=mesh['row'=8,'col'=4] {'col'}, use_global_device_ids=true, to_apply=%region_15.0 | all-reduce | flops 128 | bytes 1024 | tf_op jit(solution)/shard_map/psum | solution.py:96
  421.8 0.6 broadcast_multiply_fusion.2
  422.5 8.7 %broadcast_multiply_fusion = f32[1536,1536]{1,0:T(8,128)} fusion(f32[1536,1536]{1,0:T(8,128)} %get-tuple-element.31, f32[]{:T(128)S(6)} %min.3), kind=kLoop, calls=%fused_computation.3 | loop fusion | flops 2359296 | bytes 18874372 | tf_op jit(solution)/shard_map/mul | solution.py:111
  431.1 0.0 slice-done
  431.1 0.0 slice-done.1
  431.1 0.0 slice-done.2
  431.1 0.0 copy-start.1
  431.2 0.0 copy-start.2
  431.2 0.0 copy-start.3
  431.2 4.8 %broadcast_multiply_fusion.1 = f32[1536,1536]{1,0:T(8,128)} fusion(f32[1536,1536]{1,0:T(8,128)S(1)} %bitcast.15, f32[]{:T(128)S(6)} %min.3), kind=kLoop, calls=%fused_computation.4 | loop fusion | flops 2359296 | bytes 18874372 | tf_op jit(solution)/shard_map/mul | solution.py:111
  436.0 0.0 copy-done.1
  436.0 1.7 fusion.23
  437.7 0.0 copy-done.3
  437.7 0.9 fusion.16
  (13 shorter events, 0.0 us)
Async XLA Ops:
  7.2 30.5 %all-gather.13.cloned.1.call-start = ((), (), s32[]{:S(2)}) async-start(), calls=%async_computation.9 | async-start | bytes 1769472 | tf_op jit(solution)/shard_map/all_gather | solution.py:82
  7.9 56.4 %all-gather.7.cloned.1.call-start = ((), (), s32[]{:S(2)}) async-start(), calls=%async_computation.4 | async-start | bytes 1769472 | tf_op jit(solution)/shard_map/all_gather | solution.py:45
  23.6 67.3 %all-gather.9.cloned.1.call-start = ((), (), s32[]{:S(2)}) async-start(), calls=%async_computation.5 | async-start | bytes 1769472 | tf_op jit(solution)/shard_map/all_gather | solution.py:46
  24.3 113.1 %reduce-scatter.9.cloned.1.call-start = ((), (), s32[]{:S(2)}) async-start(), calls=%async_computation.10 | async-start | bytes 3932160 | tf_op jit(solution)/shard_map/reduce_scatter | solution.py:83
  44.8 166.1 %reduce-scatter.5.cloned.1.call-start = ((), (), s32[]{:S(2)}) async-start(), calls=%async_computation.6 | async-start | bytes 7864320 | tf_op jit(solution)/shard_map/reduce_scatter | solution.py:49
  99.1 145.8 %all-gather.15.cloned.1.call-start = ((), (), s32[]{:S(2)}) async-start(), calls=%async_computation.11 | async-start | bytes 1966080 | tf_op jit(solution)/shard_map/all_gather | solution.py:88
  213.9 63.7 %all-gather.11.cloned.1.call-start = ((), (), s32[]{:S(2)}) async-start(), calls=%async_computation.7 | async-start | bytes 1966080 | tf_op jit(solution)/shard_map/all_gather | solution.py:75
  214.7 96.2 %all-gather.17.cloned.1.call-start = ((), (), s32[]{:S(2)}) async-start(), calls=%async_computation.13 | async-start | bytes 1966080 | tf_op jit(solution)/shard_map/all_gather | solution.py:87
  215.4 138.2 %reduce-scatter.11.cloned.1.call-start = ((), (), s32[]{:S(2)}) async-start(), calls=%async_computation.12 | async-start | bytes 3538944 | tf_op jit(solution)/shard_map/reduce_scatter | solution.py:92
  252.1 183.9 %reduce-scatter.7.cloned.1.call-start = ((), (), s32[]{:S(2)}) async-start(), calls=%async_computation.8 | async-start | bytes 3538944 | tf_op jit(solution)/shard_map/reduce_scatter | solution.py:79
  284.8 1.4 copy-start.5
  284.8 1.9 copy-start.6
  292.7 60.9 %copy-start = (bf16[64,1536]{1,0:T(8,128)(2,1)S(1)}, bf16[64,1536]{1,0:T(8,128)(2,1)}, u32[]{:S(2)}) copy-start(bf16[64,1536]{1,0:T(8,128)(2,1)} %param.7) | copy-start | bytes 589828
  292.7 60.9 %copy-start.4 = (f32[1536]{0:T(1024)S(1)}, f32[1536]{0:T(1024)}, u32[]{:S(2)}) copy-start(f32[1536]{0:T(1024)} %param.9) | copy-start | bytes 18436
  353.6 77.5 %slice-start = ((s8[9437184]{0:T(1024)(128)(4,1)}), s8[1048576]{0:T(1024)(128)(4,1)S(1)}, s32[]{:S(2)}) async-start(s8[9437184]{0:T(1024)(128)(4,1)} %bitcast.14), calls=%async_computation.14 | async-start | bytes 2097152
  422.4 8.7 %slice-start.1 = ((s8[9437184]{0:T(1024)(128)(4,1)}), s8[4194304]{0:T(1024)(128)(4,1)S(1)}, s32[]{:S(2)}) async-start(s8[9437184]{0:T(1024)(128)(4,1)} %bitcast.14), calls=%async_computation.15 | async-start | bytes 8388608
  422.4 8.7 %slice-start.2 = ((s8[9437184]{0:T(1024)(128)(4,1)}), s8[4194304]{0:T(1024)(128)(4,1)S(1)}, s32[]{:S(2)}) async-start(s8[9437184]{0:T(1024)(128)(4,1)} %bitcast.14), calls=%async_computation.16 | async-start | bytes 8388608
  431.1 4.8 %copy-start.1 = (bf16[64,1536]{1,0:T(8,128)(2,1)S(1)}, bf16[64,1536]{1,0:T(8,128)(2,1)}, u32[]{:S(2)}) copy-start(bf16[64,1536]{1,0:T(8,128)(2,1)} %param.6) | copy-start | bytes 589828
  431.2 6.5 %copy-start.2 = (f32[64,1536]{1,0:T(8,128)S(1)}, f32[64,1536]{1,0:T(8,128)}, u32[]{:S(2)}) copy-start(f32[64,1536]{1,0:T(8,128)} %reduce-scatter.11.cloned.1.call-done) | copy-start | bytes 1179652
  431.2 6.5 %copy-start.3 = (bf16[64,1536]{1,0:T(8,128)(2,1)S(1)}, bf16[64,1536]{1,0:T(8,128)(2,1)}, u32[]{:S(2)}) copy-start(bf16[64,1536]{1,0:T(8,128)(2,1)} %param.8) | copy-start | bytes 589828
Sparse Core Ops, SparseCore 0:
  9.6 27.9 all-gather.12
  39.8 24.3 all-gather.6
  66.5 24.3 all-gather.8
  94.3 43.0 reduce-scatter.8
  140.8 70.0 reduce-scatter.4
  214.0 30.8 all-gather.14
  246.8 30.8 all-gather.10
  280.0 30.8 all-gather.16
  313.2 40.3 reduce-scatter.10
  355.8 40.2 reduce-scatter.6
where the time goes:
time: 447 us
  waiting for transfers between devices  274 us (61%)
  blocking collectives  76.2 us (17%)
  matrix products  46.1 us (10%)
  other arithmetic  29.2 us (7%)
  between operations  18.1 us (4%)
    reduce_scatter x1, waiting for transfers between devices, up_both(): lax.psum_scatter(jnp.concatenate([jnp.dot(full_a, w_up, preferred_element...  73.5 us
    psum x1, blocking collectives, on_device(): lax.psum(weight_squares + first_row * jnp.sum(g_gain * g_gain), ('row', '...  38.8 us
    reduce_scatter x1, waiting for transfers between devices, on_device(): lax.psum_scatter(contract(grad_full, w_down, 1, 1), 'col', scatter_dimens...  38.2 us
    reduce_scatter x1, waiting for transfers between devices, on_device(): lax.psum_scatter(input_total, 'row', scatter_dimension=0, tiled=True)  32.5 us
    all_gather x1, waiting for transfers between devices, on_device(): pre_piece = lax.all_gather(grad_pre, 'col', axis=0, tiled=True)  29.5 us
    dot_general x4, matrix products, contract(): lax.dot_general(left, right, (((left_dim,), (right_dim,)), ((), ())), pre...  29.2 us
    all_gather x1, waiting for transfers between devices, on_device(): lax.all_gather(hidden_a, 'col', axis=0, tiled=True)  25.3 us
    all_gather x1, waiting for transfers between devices, up_both(): lax.all_gather(normed_b, 'row', axis=0, tiled=True)  21.7 us
  transfers between devices with their start and end apart: 10, of which 9 were waited for; matrix products, arithmetic and copies ran while one was open for 16% of the time, Pallas kernels for 0%

commit v1 on v0

--- a/solution.py
+++ b/solution.py
@@ -103,7 +103,7 @@
     weight_squares = jnp.sum(up_total * up_total) + jnp.sum(down_total * down_total)
     g_gain = lax.psum(gain_part, "row")
     first_row = (lax.axis_index("row") == 0).astype(jnp.float32)
-    total = lax.psum(weight_squares + first_row * jnp.sum(g_gain * g_gain), ("row", "col"))
+    total = lax.psum(lax.psum(weight_squares + first_row * jnp.sum(g_gain * g_gain), "row"), "col")
     param_count = 2 * D * FF + D
     norm_value = jnp.sqrt(total)
     grad_rms = norm_value / math.sqrt(param_count)

time: 447 us -> 424 us (0.949)
  blocking collectives: 76.2 us -> 52.7 us
    psum x1, blocking collectives: 38.8 us -> 14.6 us  [on_device(): lax.psum(weight_squares + first_row * jnp.sum(g_gain * g_gain), 'row')]
where the time goes in v1:
time: 424 us; the launch traced here: 423 us
  waiting for transfers between devices  275 us (65%)
  blocking collectives  52.7 us (12%)
  matrix products  45.9 us (11%)
  other arithmetic  29.2 us (7%)
  between operations  18.1 us (4%)
    reduce_scatter x1, waiting for transfers between devices, up_both(): lax.psum_scatter(jnp.concatenate([jnp.dot(full_a, w_up, preferred_element...  73.5 us
    reduce_scatter x1, waiting for transfers between devices, on_device(): lax.psum_scatter(contract(grad_full, w_down, 1, 1), 'col', scatter_dimens...  38.2 us
    reduce_scatter x1, waiting for transfers between devices, on_device(): lax.psum_scatter(input_total, 'row', scatter_dimension=0, tiled=True)  33.2 us
    all_gather x1, waiting for transfers between devices, on_device(): pre_piece = lax.all_gather(grad_pre, 'col', axis=0, tiled=True)  29.5 us
    dot_general x4, matrix products, contract(): lax.dot_general(left, right, (((left_dim,), (right_dim,)), ((), ())), pre...  29 us
    all_gather x1, waiting for transfers between devices, on_device(): lax.all_gather(hidden_a, 'col', axis=0, tiled=True)  25.3 us
    all_gather x1, waiting for transfers between devices, up_both(): lax.all_gather(normed_a, 'row', axis=0, tiled=True)  21.7 us
    all_gather x1, waiting for transfers between devices, up_both(): lax.all_gather(normed_b, 'row', axis=0, tiled=True)  19.5 us
  transfers between devices with their start and end apart: 10, of which 9 were waited for; matrix products, arithmetic and copies ran while one was open for 16% of the time, Pallas kernels for 0%

profile of v1, /device:TPU:0, one launch (start us, length us, event | category | flops | bytes accessed | tf_op | source)
XLA Modules:
  0.0 423.1 jit_solution(14734123398345530264)
XLA Ops:
  7.2 0.0 all-gather.13.cloned.1.call-start
  7.2 0.7 all-gather.13.cloned.1.call-update
  7.9 0.0 all-gather.9.cloned.1.call-start
  7.9 1.1 convert_reduce_fusion.1
  9.0 1.1 convert_reduce_fusion
  10.1 11.4 %all-reduce.1 = (f32[64]{0:T(128)S(1)}, f32[64]{0:T(128)S(1)}, f32[64]{0:T(128)S(1)}, f32[64]{0:T(128)S(1)}) all-reduce(f32[64]{0:T(128)S(1)} %get-tuple-element.12, f32[64]{0:T(128)S(1)} %get-tuple-element.11, f32[64]{0:T(128)S(1)} %get-tuple-element.10, f32[64]{0:T(128)S(1)} %get-tuple-element.9), channel_id=1, replica_groups=mesh['row'=8,'col'=4] {'col'}, use_global_device_ids=true, to_apply=%region_7.0 | all-reduce | flops 256 | bytes 2048 | tf_op jit(solution)/shard_map/psum | solution.py:67
  21.5 2.0 fusion.21
  23.6 0.0 all-gather.9.cloned.1.call-update
  23.6 0.0 all-gather.7.cloned.1.call-start
  23.6 0.7 all-gather.7.cloned.1.call-update
  24.3 0.0 reduce-scatter.9.cloned.1.call-start
  24.4 13.3 %all-gather.13.cloned.1.call-done = bf16[512,1536]{1,0:T(8,128)(2,1)} async-done(((bf16[64,1536]{1,0:T(8,128)(2,1)}), bf16[512,1536]{1,0:T(8,128)(2,1)}) %all-gather.13.cloned.1.call-update) | async-done | bytes 1572880 | tf_op jit(solution)/shard_map/all_gather | solution.py:82
  37.6 7.1 %fusion.27 = f32[512,1536]{1,0:T(8,128)} fusion(bf16[512,1536]{1,0:T(8,128)(2,1)} %all-gather.13.cloned.1.call-done, bf16[1536,1536]{1,0:T(8,128)(2,1)} %param.11), kind=kOutput, calls=%fused_computation.52 | convolution fusion | flops 2415919104 | bytes 9437184 | tf_op jit(solution)/shard_map/dot_general | solution.py:25
  44.8 0.0 reduce-scatter.9.cloned.1.call-update
  44.8 0.0 reduce-scatter.5.cloned.1.call-start
  44.8 19.5 %all-gather.9.cloned.1.call-done = bf16[512,1536]{1,0:T(8,128)(2,1)} async-done(((bf16[64,1536]{1,0:T(8,128)(2,1)}), bf16[512,1536]{1,0:T(8,128)(2,1)}) %all-gather.9.cloned.1.call-update) | async-done | bytes 1572880 | tf_op jit(solution)/shard_map/all_gather | solution.py:46
  64.3 4.9 %fusion.25 = f32[512,1536]{1,0:T(8,128)S(1)} fusion(bf16[512,1536]{1,0:T(8,128)(2,1)} %all-gather.9.cloned.1.call-done, bf16[1536,1536]{1,0:T(8,128)(2,1)} %param.10), kind=kOutput, calls=%fused_computation.50 | convolution fusion | flops 2415919104 | bytes 9437184 | tf_op jit(solution)/shard_map/dot_general | solution.py:53
  69.2 21.7 %all-gather.7.cloned.1.call-done = bf16[512,1536]{1,0:T(8,128)(2,1)} async-done(((bf16[64,1536]{1,0:T(8,128)(2,1)}), bf16[512,1536]{1,0:T(8,128)(2,1)}) %all-gather.7.cloned.1.call-update) | async-done | bytes 1572880 | tf_op jit(solution)/shard_map/all_gather | solution.py:45
  90.9 4.9 %fusion.24 = f32[512,1536]{1,0:T(8,128)S(1)} fusion(bf16[512,1536]{1,0:T(8,128)(2,1)} %all-gather.7.cloned.1.call-done, bf16[1536,1536]{1,0:T(8,128)(2,1)} %param.10), kind=kOutput, calls=%fused_computation.49 | convolution fusion | flops 2415919104 | bytes 9437184 | tf_op jit(solution)/shard_map/dot_general | solution.py:52
  95.8 3.3 pad_maximum_fusion
  99.1 0.0 reduce-scatter.5.cloned.1.call-update
  99.1 0.0 all-gather.15.cloned.1.call-start
  99.2 38.2 %reduce-scatter.9.cloned.1.call-done = f32[128,1536]{1,0:T(8,128)} async-done(((f32[512,1536]{1,0:T(8,128)}), f32[128,1536]{1,0:T(8,128)}) %reduce-scatter.9.cloned.1.call-update) | async-done | bytes 786448 | tf_op jit(solution)/shard_map/reduce_scatter | solution.py:83
  137.4 73.5 %reduce-scatter.5.cloned.1.call-done = f32[128,3072]{1,0:T(8,128)} async-done(((f32[512,3072]{1,0:T(8,128)}), f32[128,3072]{1,0:T(8,128)}) %reduce-scatter.5.cloned.1.call-update) | async-done | bytes 1572880 | tf_op jit(solution)/shard_map/reduce_scatter | solution.py:49
  210.9 3.0 multiply_convert_fusion
  213.9 0.0 all-gather.15.cloned.1.call-update
  213.9 0.0 all-gather.11.cloned.1.call-start
  214.0 0.7 all-gather.11.cloned.1.call-update
  214.7 0.0 all-gather.17.cloned.1.call-start
  214.7 0.7 all-gather.17.cloned.1.call-update
  215.4 0.0 reduce-scatter.11.cloned.1.call-start
  215.5 29.5 %all-gather.15.cloned.1.call-done = bf16[512,1536]{1,0:T(8,128)(2,1)} async-done(((bf16[128,1536]{1,0:T(8,128)(2,1)}), bf16[512,1536]{1,0:T(8,128)(2,1)}) %all-gather.15.cloned.1.call-update) | async-done | bytes 1572880 | tf_op jit(solution)/shard_map/all_gather | solution.py:88
  244.9 7.1 %fusion.28 = f32[512,1536]{1,0:T(8,128)} fusion(bf16[512,1536]{1,0:T(8,128)(2,1)} %all-gather.15.cloned.1.call-done, bf16[1536,1536]{1,0:T(8,128)(2,1)} %param.10), kind=kOutput, calls=%fused_computation.53 | convolution fusion | flops 2415919104 | bytes 9437184 | tf_op jit(solution)/shard_map/dot_general | solution.py:25
  252.1 0.0 reduce-scatter.11.cloned.1.call-update
  252.1 0.2 reduce-scatter.7.cloned.1.call-start
  252.3 25.3 %all-gather.11.cloned.1.call-done = bf16[512,1536]{1,0:T(8,128)(2,1)} async-done(((bf16[128,1536]{1,0:T(8,128)(2,1)}), bf16[512,1536]{1,0:T(8,128)(2,1)}) %all-gather.11.cloned.1.call-update) | async-done | bytes 1572880 | tf_op jit(solution)/shard_map/all_gather | solution.py:75
  277.7 7.0 %fusion.26 = f32[512,1536]{1,0:T(8,128)} fusion(bf16[512,1536]{1,0:T(8,128)(2,1)} %all-gather.11.cloned.1.call-done, bf16[1536,1536]{1,0:T(8,128)(2,1)} %param.11), kind=kOutput, calls=%fused_computation.51 | convolution fusion | flops 2415919104 | bytes 9437184 | tf_op jit(solution)/shard_map/dot_general | solution.py:74
  284.7 0.0 reduce-scatter.7.cloned.1.call-update
  284.7 1.4 copy-done.5
  286.2 0.6 copy-done.6
  286.7 6.0 %multiply_reduce_fusion.1 = (f32[]{:T(128)}, f32[1536,1536]{1,0:T(8,128)}) fusion(bf16[512,1536]{1,0:T(8,128)(2,1)S(1)} %copy-done.5, bf16[512,1536]{1,0:T(8,128)(2,1)S(1)} %copy-done.6), kind=kOutput, calls=%fused_computation.1 | convolution fusion | flops 2420637696 | bytes 12582916 | tf_op jit(solution)/shard_map/dot_general | solution.py:25
  292.8 17.6 %all-gather.17.cloned.1.call-done = bf16[512,1536]{1,0:T(8,128)(2,1)} async-done(((bf16[128,1536]{1,0:T(8,128)(2,1)}), bf16[512,1536]{1,0:T(8,128)(2,1)}) %all-gather.17.cloned.1.call-update) | async-done | bytes 1572880 | tf_op jit(solution)/shard_map/all_gather | solution.py:87
  310.4 8.8 %multiply_reduce_fusion = (f32[]{:T(128)}, f32[1536,1536]{1,0:T(8,128)}) fusion(bf16[512,1536]{1,0:T(8,128)(2,1)} %all-gather.17.cloned.1.call-done, bf16[512,1536]{1,0:T(8,128)(2,1)} %all-gather.13.cloned.1.call-done), kind=kOutput, calls=%fused_computation | convolution fusion | flops 2420637696 | bytes 12582916 | tf_op jit(solution)/shard_map/dot_general | solution.py:25
  320.4 33.2 %reduce-scatter.11.cloned.1.call-done = f32[64,1536]{1,0:T(8,128)} async-done(((f32[512,1536]{1,0:T(8,128)}), f32[64,1536]{1,0:T(8,128)}) %reduce-scatter.11.cloned.1.call-update) | async-done | bytes 393232 | tf_op jit(solution)/shard_map/reduce_scatter | solution.py:92
  353.6 0.0 copy-done
  353.6 0.0 copy-done.4
  353.7 1.4 fusion.17
  355.0 16.1 %psum.69 = f32[1536]{0:T(1024)S(1)} all-reduce(f32[1536]{0:T(1024)S(1)} %get-tuple-element.6), channel_id=1, replica_groups=mesh['row'=8,'col'=4] {'row'}, use_global_device_ids=true, to_apply=%region_19.0 | all-reduce | flops 1536 | bytes 12288 | tf_op jit(solution)/shard_map/psum | solution.py:104
  371.1 0.6 multiply_reduce_fusion.3
  372.3 14.6 %psum.70 = f32[]{:T(128)} all-reduce(f32[]{:T(128)S(6)} %add.62), channel_id=1, replica_groups=mesh['row'=8,'col'=4] {'row'}, use_global_device_ids=true, to_apply=%region_21.0 | all-reduce | flops 1 | bytes 8 | tf_op jit(solution)/shard_map/psum | solution.py:106
  387.0 10.6 %all-reduce = (f32[64]{0:T(128)S(1)}, f32[64]{0:T(128)S(1)}, f32[]{:T(128)}) all-reduce(f32[64]{0:T(128)S(1)} %get-tuple-element.7, f32[64]{0:T(128)S(1)} %get-tuple-element.8, f32[]{:T(128)} %psum.70), channel_id=1, replica_groups=mesh['row'=8,'col'=4] {'col'}, use_global_device_ids=true, to_apply=%region_15.0 | all-reduce | flops 129 | bytes 1032 | tf_op jit(solution)/shard_map/psum | solution.py:96
  398.3 0.6 broadcast_multiply_fusion.2
  399.0 8.7 %broadcast_multiply_fusion.1 = f32[1536,1536]{1,0:T(8,128)} fusion(f32[1536,1536]{1,0:T(8,128)} %get-tuple-element.30, f32[]{:T(128)S(6)} %min.3), kind=kLoop, calls=%fused_computation.4 | loop fusion | flops 2359296 | bytes 18874372 | tf_op jit(solution)/shard_map/mul | solution.py:111
  407.6 0.0 slice-done
  407.6 0.0 slice-done.1
  407.6 0.0 slice-done.2
  407.6 0.0 copy-start.1
  407.7 0.0 copy-start.2
  407.7 0.0 copy-start.3
  407.7 4.8 %broadcast_multiply_fusion = f32[1536,1536]{1,0:T(8,128)} fusion(f32[1536,1536]{1,0:T(8,128)S(1)} %bitcast.15, f32[]{:T(128)S(6)} %min.3), kind=kLoop, calls=%fused_computation.3 | loop fusion | flops 2359296 | bytes 18874372 | tf_op jit(solution)/shard_map/mul | solution.py:111
  412.5 0.0 copy-done.1
  412.5 1.7 fusion.23
  414.2 0.0 copy-done.2
  414.2 0.9 fusion.16
  (13 shorter events, 0.0 us)
Async XLA Ops:
  7.2 30.5 %all-gather.13.cloned.1.call-start = ((), (), s32[]{:S(2)}) async-start(), calls=%async_computation.9 | async-start | bytes 1769472 | tf_op jit(solution)/shard_map/all_gather | solution.py:82
  7.9 56.4 %all-gather.9.cloned.1.call-start = ((), (), s32[]{:S(2)}) async-start(), calls=%async_computation.5 | async-start | bytes 1769472 | tf_op jit(solution)/shard_map/all_gather | solution.py:46
  23.6 67.3 %all-gather.7.cloned.1.call-start = ((), (), s32[]{:S(2)}) async-start(), calls=%async_computation.4 | async-start | bytes 1769472 | tf_op jit(solution)/shard_map/all_gather | solution.py:45
  24.3 113.1 %reduce-scatter.9.cloned.1.call-start = ((), (), s32[]{:S(2)}) async-start(), calls=%async_computation.10 | async-start | bytes 3932160 | tf_op jit(solution)/shard_map/reduce_scatter | solution.py:83
  44.8 166.1 %reduce-scatter.5.cloned.1.call-start = ((), (), s32[]{:S(2)}) async-start(), calls=%async_computation.6 | async-start | bytes 7864320 | tf_op jit(solution)/shard_map/reduce_scatter | solution.py:49
  99.1 145.8 %all-gather.15.cloned.1.call-start = ((), (), s32[]{:S(2)}) async-start(), calls=%async_computation.11 | async-start | bytes 1966080 | tf_op jit(solution)/shard_map/all_gather | solution.py:88
  213.9 63.7 %all-gather.11.cloned.1.call-start = ((), (), s32[]{:S(2)}) async-start(), calls=%async_computation.7 | async-start | bytes 1966080 | tf_op jit(solution)/shard_map/all_gather | solution.py:75
  214.7 95.7 %all-gather.17.cloned.1.call-start = ((), (), s32[]{:S(2)}) async-start(), calls=%async_computation.13 | async-start | bytes 1966080 | tf_op jit(solution)/shard_map/all_gather | solution.py:87
  215.4 138.2 %reduce-scatter.11.cloned.1.call-start = ((), (), s32[]{:S(2)}) async-start(), calls=%async_computation.12 | async-start | bytes 3538944 | tf_op jit(solution)/shard_map/reduce_scatter | solution.py:92
  252.1 160.4 %reduce-scatter.7.cloned.1.call-start = ((), (), s32[]{:S(2)}) async-start(), calls=%async_computation.8 | async-start | bytes 3538944 | tf_op jit(solution)/shard_map/reduce_scatter | solution.py:79
  284.7 1.4 copy-start.5
  284.7 2.0 copy-start.6
  292.8 60.9 %copy-start = (bf16[64,1536]{1,0:T(8,128)(2,1)S(1)}, bf16[64,1536]{1,0:T(8,128)(2,1)}, u32[]{:S(2)}) copy-start(bf16[64,1536]{1,0:T(8,128)(2,1)} %param.7) | copy-start | bytes 589828
  292.8 60.9 %copy-start.4 = (f32[1536]{0:T(1024)S(1)}, f32[1536]{0:T(1024)}, u32[]{:S(2)}) copy-start(f32[1536]{0:T(1024)} %param.9) | copy-start | bytes 18436
  353.7 54.0 %slice-start = ((s8[9437184]{0:T(1024)(128)(4,1)}), s8[1048576]{0:T(1024)(128)(4,1)S(1)}, s32[]{:S(2)}) async-start(s8[9437184]{0:T(1024)(128)(4,1)} %bitcast.14), calls=%async_computation.14 | async-start | bytes 2097152
  399.0 8.7 %slice-start.1 = ((s8[9437184]{0:T(1024)(128)(4,1)}), s8[4194304]{0:T(1024)(128)(4,1)S(1)}, s32[]{:S(2)}) async-start(s8[9437184]{0:T(1024)(128)(4,1)} %bitcast.14), calls=%async_computation.15 | async-start | bytes 8388608
  399.0 8.7 %slice-start.2 = ((s8[9437184]{0:T(1024)(128)(4,1)}), s8[4194304]{0:T(1024)(128)(4,1)S(1)}, s32[]{:S(2)}) async-start(s8[9437184]{0:T(1024)(128)(4,1)} %bitcast.14), calls=%async_computation.16 | async-start | bytes 8388608
  407.6 4.8 %copy-start.1 = (bf16[64,1536]{1,0:T(8,128)(2,1)S(1)}, bf16[64,1536]{1,0:T(8,128)(2,1)}, u32[]{:S(2)}) copy-start(bf16[64,1536]{1,0:T(8,128)(2,1)} %param.6) | copy-start | bytes 589828
  407.7 6.5 %copy-start.2 = (f32[64,1536]{1,0:T(8,128)S(1)}, f32[64,1536]{1,0:T(8,128)}, u32[]{:S(2)}) copy-start(f32[64,1536]{1,0:T(8,128)} %reduce-scatter.11.cloned.1.call-done) | copy-start | bytes 1179652
  407.7 6.5 %copy-start.3 = (bf16[64,1536]{1,0:T(8,128)(2,1)S(1)}, bf16[64,1536]{1,0:T(8,128)(2,1)}, u32[]{:S(2)}) copy-start(bf16[64,1536]{1,0:T(8,128)(2,1)} %param.8) | copy-start | bytes 589828
Sparse Core Ops, SparseCore 0:
  9.6 27.9 all-gather.12
  39.8 24.3 all-gather.8
  66.5 24.3 all-gather.6
  94.3 43.0 reduce-scatter.8
  140.8 70.0 reduce-scatter.4
  214.1 30.8 all-gather.14
  246.8 30.8 all-gather.10
  279.5 30.8 all-gather.16
  313.2 40.3 reduce-scatter.10
  355.8 40.0 reduce-scatter.6
